TPU v7x, 256 devices: a 8x8x2 block of a 8x8x16 slice. The times are simulated.
256 devices in a mesh: groups: 2 (over z), dap: 128 (over x, y, core).
Axes of the slice: x: 8, y: 8, z: 2, core: 2. Of those that a mesh axis runs over, the one named last changes fastest.
The devices are a block of a 8x8x16 slice.
Arguments:
- homolog_tensor: bfloat16 [1024, 256, 256], P(('groups', 'dap')), parts along dimension 0, may hold values from -1 to 1
- couple_tensor: bfloat16 [512, 256, 128], P(('groups', 'dap')), parts along dimension 0, may hold values from -6 to 6
- horizontal_drop_filter: int32 [512, 256], P('groups'), parts along dimension 0, may hold values 0 or 1
- couple_offset_matrix: bfloat16 [128, 8], replicated, may hold values from -0.29882812 to 0.29882812
- horizontal_attend_matrix: bfloat16 [256, 1024], replicated, may hold values from -0.375 to 0.375
- horizontal_exit_matrix: bfloat16 [256, 256], replicated, may hold values from -0.375 to 0.375
- vertical_attend_matrix: bfloat16 [256, 1024], replicated, may hold values from -0.375 to 0.375
- vertical_exit_matrix: bfloat16 [256, 256], replicated, may hold values from -0.375 to 0.375
- averaged_product_flanks: bfloat16 [256, 64], replicated, may hold values from -0.375 to 0.375
- averaged_product_exit: bfloat16 [1024, 128], replicated, may hold values from -1 to 1
Outputs:
- alignment_output: bfloat16 [1024, 256, 256], P('groups', 'dap'), parts along dimension 0
- pair_output_state: bfloat16 [512, 256, 128], P(('groups', 'dap')), parts along dimension 0
There are 2 independent parts, one for each index of `groups`. A program takes and returns all parts, laid end to end along the dimension named above; an argument that names none is the same for every part. Nothing has to cross between parts.
All inputs are finite; a program needn't handle non-finite values.
Results may differ from a plain program's by a relative error of at most 0.012.
Values may be sent and summed in bfloat16 or wider, within the bound.
A program may use at most 64 MiB of HBM per device.

v0:
```python
import jax
import jax.numpy as jnp
from jax import lax
from jax.sharding import Mesh
from jax.sharding import PartitionSpec as P

HEAD_NUMBER = 8
HEAD_WIDTH = 32
FACTOR_FEATURES = 32
DAP = ("dap_0", "dap_1", "dap_2")
GROUPS_DAP = ("groups", "dap_0", "dap_1", "dap_2")


def joined_along(tiles, dim):
    tiles = jnp.moveaxis(tiles, 0, dim)
    dims = tiles.shape
    return tiles.reshape(*dims[:dim], dims[dim] * dims[dim + 1], *dims[dim + 2 :])


def stacked_from(shard, axes, order):
    tiles = shard[None]
    for k in order:
        tiles = lax.all_gather(tiles, axes[k], axis=0, tiled=True)
    carried = [lax.axis_size(axes[k]) for k in reversed(order)]
    tiles = tiles.reshape(*carried, *shard.shape)
    turned = sorted(range(len(order)), key=lambda place: order[len(order) - 1 - place])
    return tiles.transpose(*turned, *range(len(order), tiles.ndim)).reshape(-1, *shard.shape)


def gather_axes(shard, axes, order, dim):
    return joined_along(stacked_from(shard, axes, order), dim)


def standardise_features(values):
    values = values.astype(jnp.float32)
    center = values - jnp.mean(values, axis=-1, keepdims=True)
    spread = jnp.mean(center * center, axis=-1, keepdims=True)
    return center * lax.rsqrt(spread + 1e-05)


def attend(normed, w_qkvg, w_out, bias):
    batch, length = (normed.shape[0], normed.shape[1])
    proj = jnp.einsum("blc,cf->blf", normed, w_qkvg, preferred_element_type=jnp.float32)
    proj = proj.reshape(batch, length, 4, HEAD_NUMBER, HEAD_WIDTH)
    query = (proj[:, :, 0] * HEAD_WIDTH ** (-0.5)).astype(jnp.bfloat16)
    keys = proj[:, :, 1].astype(jnp.bfloat16)
    values = proj[:, :, 2].astype(jnp.bfloat16)
    gate = proj[:, :, 3]
    if bias is None:
        bias = jnp.zeros((HEAD_NUMBER, length, length), jnp.bfloat16)

    def one_head(items):
        qh, kh, vh, bh = items
        scores = jnp.einsum("bid,bjd->bij", qh, kh, preferred_element_type=jnp.float32)
        scores = scores + bh.astype(jnp.float32)[None]
        weights = jax.nn.softmax(scores, axis=-1).astype(jnp.bfloat16)
        return jnp.einsum("bij,bjd->bid", weights, vh, preferred_element_type=jnp.float32)

    heads = lax.map(
        one_head,
        (jnp.moveaxis(query, 2, 0), jnp.moveaxis(keys, 2, 0), jnp.moveaxis(values, 2, 0), bias),
    )
    heads = jnp.moveaxis(heads, 0, 2)
    gated = (
        (jax.nn.sigmoid(gate) * heads)
        .astype(jnp.bfloat16)
        .reshape(batch, length, HEAD_NUMBER * HEAD_WIDTH)
    )
    return jnp.einsum("blk,kc->blc", gated, w_out, preferred_element_type=jnp.float32)


def shards(
    homolog_tensor,
    couple_tensor,
    horizontal_drop_filter,
    couple_offset_matrix,
    horizontal_attend_matrix,
    horizontal_exit_matrix,
    vertical_attend_matrix,
    vertical_exit_matrix,
    averaged_product_flanks,
    averaged_product_exit,
):
    normed_pair = standardise_features(couple_tensor).astype(jnp.bfloat16)
    own_bias = jnp.einsum(
        "ijz,zh->hij", normed_pair, couple_offset_matrix, preferred_element_type=jnp.float32
    ).astype(jnp.bfloat16)
    bias = gather_axes(own_bias, DAP, (0, 1, 2), 1)
    starting_answer = standardise_features(homolog_tensor).astype(jnp.bfloat16)
    perform_refresh = attend(
        starting_answer, horizontal_attend_matrix, horizontal_exit_matrix, bias
    )
    homolog_later = (
        homolog_tensor.astype(jnp.float32)
        + horizontal_drop_filter.astype(jnp.float32) * (1.0 / 0.9) * perform_refresh
    ).astype(jnp.bfloat16)
    incoming_blocks = lax.all_to_all(homolog_later, DAP, split_axis=1, concat_axis=0, tiled=True)
    column_layout = jnp.swapaxes(incoming_blocks, 0, 1)
    perform_refresh = attend(
        standardise_features(column_layout).astype(jnp.bfloat16),
        vertical_attend_matrix,
        vertical_exit_matrix,
        None,
    )
    alignment_output = jnp.swapaxes(
        (column_layout.astype(jnp.float32) + perform_refresh).astype(jnp.bfloat16), 0, 1
    )
    final_result = standardise_features(alignment_output).astype(jnp.bfloat16)
    factors = jnp.einsum(
        "sic,cf->sif", final_result, averaged_product_flanks, preferred_element_type=jnp.float32
    )
    left = factors[..., :FACTOR_FEATURES].astype(jnp.bfloat16)
    right = factors[..., FACTOR_FEATURES:].astype(jnp.bfloat16)
    total = left.shape[0]
    own_rows = left.shape[1]
    piece = lax.all_gather(right, DAP, axis=1, tiled=True)
    outer = jnp.einsum("sic,sjd->ijcd", left, piece, preferred_element_type=jnp.float32) / total
    outer = outer.astype(jnp.bfloat16).reshape(
        own_rows, piece.shape[1], FACTOR_FEATURES * FACTOR_FEATURES
    )
    change = jnp.einsum(
        "ijk,kz->ijz", outer, averaged_product_exit, preferred_element_type=jnp.float32
    )
    pair_output_state = (couple_tensor.astype(jnp.float32) + change).astype(jnp.bfloat16)
    return (alignment_output, pair_output_state)


def solution(mesh):
    torus = Mesh(
        mesh.devices.reshape(mesh.shape["groups"], 8, 8, 2), ("groups", "dap_0", "dap_1", "dap_2")
    )
    return jax.shard_map(
        shards,
        mesh=torus,
        in_specs=(
            P(GROUPS_DAP, None, None),
            P(GROUPS_DAP, None, None),
            P("groups", None),
            P(),
            P(),
            P(),
            P(),
            P(),
            P(),
            P(),
        ),
        out_specs=(P("groups", DAP, None), P(GROUPS_DAP, None, None)),
        check_vma=False,
    )
```

profile of v0, /device:TPU:513, one launch (start us, length us, event | category | flops | bytes accessed | tf_op | source)
XLA Modules:
  0.0 365.0 jit_solution(12928804633516290471)
XLA Ops:
  10.7 20.9 %all-gather = bf16[64,2,256]{2,0,1:T(8,128)(2,1)S(1)} all-gather(bf16[8,2,256]{2,0,1:T(8,128)(2,1)S(1)} %fusion.37), channel_id=2, replica_groups=mesh['groups'=2,'dap_0'=8,'dap_1'=8,'dap_2'=2] {'dap_0'}, dimensions={0}, use_global_device_ids=true | all-gather | bytes 73728 | tf_op jit(solution)/shard_map/all_gather | solution.py:23
  31.7 30.9 %all_gather.13 = bf16[64,8,2,256]{3,1,0,2:T(8,128)(2,1)} all-gather(bf16[8,8,2,256]{3,1,0,2:T(8,128)(2,1)S(1)} %bitcast.194), channel_id=1, replica_groups=mesh['groups'=2,'dap_0'=8,'dap_1'=8,'dap_2'=2] {'dap_1'}, dimensions={0}, use_global_device_ids=true | all-gather | bytes 589824 | tf_op jit(solution)/shard_map/all_gather | solution.py:23
  65.3 2.0 fusion.59
  71.5 27.3 %all-gather.4.cloned.1.call-done = bf16[128,8,2,256]{3,1,0,2:T(8,128)(2,1)} async-done(((bf16[64,8,2,256]{3,1,0,2:T(8,128)(2,1)}), bf16[128,8,2,256]{3,1,0,2:T(8,128)(2,1)}) %all-gather.4.cloned.1.call-update) | async-done | bytes 1048592 | tf_op jit(solution)/shard_map/all_gather | solution.py:23
  101.0 36.0 %while.20 = (s32[]{:T(128)}, f32[8,4,256,32]{2,3,0,1:T(8,128)}, bf16[8,4,256,32]{2,3,0,1:T(8,128)(2,1)}, bf16[8,4,256,32]{2,3,0,1:T(8,128)(2,1)}, bf16[8,256,256...) while((s32[]{:T(128)}, f32[8,4,256,32]{2,3,0,1:T(8,128)}, ...), condition=%wide.region_7.8_spmd, body=%wide.region_4.7_spmd.sunk | while | flops 52233728 | bytes 4533337 | solution.py:59
  103.7 1.9 fusion.105
  108.2 1.9 fusion.105
  112.6 1.9 fusion.105
  117.1 1.8 fusion.105
  121.6 1.8 fusion.105
  126.1 1.8 fusion.105
  130.6 1.8 fusion.105
  135.1 1.9 fusion.105
  136.9 1.8 fusion.54
  141.3 14.5 %all-to-all-start = ((bf16[4,256,256]{2,0,1:T(4,128)(2,1)}), bf16[4,256,256]{2,0,1:T(4,128)(2,1)S(1)}, u32[]{:S(2)}, u32[]{:S(2)}) async-start(bf16[4,256,256]{2,0,1:T(4,128)(2,1)} %copy.59), calls=%async_computation | async-start | bytes 1048576 | tf_op jit(solution)/shard_map/all_to_all | solution.py:97
  156.1 18.9 %all-to-all-done = bf16[4,256,256]{2,0,1:T(4,128)(2,1)S(1)} async-done(((bf16[4,256,256]{2,0,1:T(4,128)(2,1)}), bf16[4,256,256]{2,0,1:T(4,128)(2,1)S(1)}, u32[]{:S(2)}, u32[]{:S(2)}) %all-to-all-start) | async-done | bytes 524320 | tf_op jit(solution)/shard_map/all_to_all | solution.py:97
  177.6 1.8 multiply_convert_fusion.1
  180.3 1.8 copy-done.1
  184.5 2.1 slice_bitcast_fusion
  186.6 73.0 %while.21 = (s32[]{:T(128)}, f32[8,2,512,32]{2,3,0,1:T(8,128)}, bf16[8,2,512,32]{2,3,0,1:T(8,128)(2,1)S(1)}, bf16[8,2,512,32]{2,3,0,1:T(8,128)(2,1)}, bf16[8,2,512,32]{2,3,0,1:T(8,128)(2,1)S(1)}, /*index=5*/s32[]{:T(128)}) while((s32[]{:T(128)}, f32[8,2,512,32]{2,3,0,1:T(8,128)}, bf16[8,2,512,32]{2,3,0,1:T(8,128)(2,1)S(1)}, ...), condition=%wide.region_13.14_spmd, body=%wide.region_10.13_spmd.sunk | while | flops 67108864 | bytes 1507417 | solution.py:59
  190.1 3.8 %dot_general.47 = f32[2,512,32]{2,1,0:T(8,128)} custom-call(bf16[2,512,32]{2,1,0:T(8,128)(2,1)} %bitcast.177, bf16[2,512,32]{2,1,0:T(8,128)(2,1)} %bitcast.176, bf16[2,512,32]{2,1,0:T(8,128)(2,1)} %bitcast.178), custom_call_target="tpu_custom_call" | custom-call | flops 67108864 | bytes 196608 | tf_op jit(solution)/shard_map/while/body/eval_jaxpr/bij,bjd->bid/dot_general | solution.py:57
  199.2 3.8 %dot_general.47 = f32[2,512,32]{2,1,0:T(8,128)} custom-call(bf16[2,512,32]{2,1,0:T(8,128)(2,1)} %bitcast.177, bf16[2,512,32]{2,1,0:T(8,128)(2,1)} %bitcast.176, bf16[2,512,32]{2,1,0:T(8,128)(2,1)} %bitcast.178), custom_call_target="tpu_custom_call" | custom-call | flops 67108864 | bytes 196608 | tf_op jit(solution)/shard_map/while/body/eval_jaxpr/bij,bjd->bid/dot_general | solution.py:57
  208.3 3.8 %dot_general.47 = f32[2,512,32]{2,1,0:T(8,128)} custom-call(bf16[2,512,32]{2,1,0:T(8,128)(2,1)} %bitcast.177, bf16[2,512,32]{2,1,0:T(8,128)(2,1)} %bitcast.176, bf16[2,512,32]{2,1,0:T(8,128)(2,1)} %bitcast.178), custom_call_target="tpu_custom_call" | custom-call | flops 67108864 | bytes 196608 | tf_op jit(solution)/shard_map/while/body/eval_jaxpr/bij,bjd->bid/dot_general | solution.py:57
  217.4 3.8 %dot_general.47 = f32[2,512,32]{2,1,0:T(8,128)} custom-call(bf16[2,512,32]{2,1,0:T(8,128)(2,1)} %bitcast.177, bf16[2,512,32]{2,1,0:T(8,128)(2,1)} %bitcast.176, bf16[2,512,32]{2,1,0:T(8,128)(2,1)} %bitcast.178), custom_call_target="tpu_custom_call" | custom-call | flops 67108864 | bytes 196608 | tf_op jit(solution)/shard_map/while/body/eval_jaxpr/bij,bjd->bid/dot_general | solution.py:57
  226.6 3.8 %dot_general.47 = f32[2,512,32]{2,1,0:T(8,128)} custom-call(bf16[2,512,32]{2,1,0:T(8,128)(2,1)} %bitcast.177, bf16[2,512,32]{2,1,0:T(8,128)(2,1)} %bitcast.176, bf16[2,512,32]{2,1,0:T(8,128)(2,1)} %bitcast.178), custom_call_target="tpu_custom_call" | custom-call | flops 67108864 | bytes 196608 | tf_op jit(solution)/shard_map/while/body/eval_jaxpr/bij,bjd->bid/dot_general | solution.py:57
  235.7 3.8 %dot_general.47 = f32[2,512,32]{2,1,0:T(8,128)} custom-call(bf16[2,512,32]{2,1,0:T(8,128)(2,1)} %bitcast.177, bf16[2,512,32]{2,1,0:T(8,128)(2,1)} %bitcast.176, bf16[2,512,32]{2,1,0:T(8,128)(2,1)} %bitcast.178), custom_call_target="tpu_custom_call" | custom-call | flops 67108864 | bytes 196608 | tf_op jit(solution)/shard_map/while/body/eval_jaxpr/bij,bjd->bid/dot_general | solution.py:57
  244.8 3.8 %dot_general.47 = f32[2,512,32]{2,1,0:T(8,128)} custom-call(bf16[2,512,32]{2,1,0:T(8,128)(2,1)} %bitcast.177, bf16[2,512,32]{2,1,0:T(8,128)(2,1)} %bitcast.176, bf16[2,512,32]{2,1,0:T(8,128)(2,1)} %bitcast.178), custom_call_target="tpu_custom_call" | custom-call | flops 67108864 | bytes 196608 | tf_op jit(solution)/shard_map/while/body/eval_jaxpr/bij,bjd->bid/dot_general | solution.py:57
  253.9 3.8 %dot_general.47 = f32[2,512,32]{2,1,0:T(8,128)} custom-call(bf16[2,512,32]{2,1,0:T(8,128)(2,1)} %bitcast.177, bf16[2,512,32]{2,1,0:T(8,128)(2,1)} %bitcast.176, bf16[2,512,32]{2,1,0:T(8,128)(2,1)} %bitcast.178), custom_call_target="tpu_custom_call" | custom-call | flops 67108864 | bytes 196608 | tf_op jit(solution)/shard_map/while/body/eval_jaxpr/bij,bjd->bid/dot_general | solution.py:57
  259.7 1.8 fusion.55
  264.1 77.3 %all-gather.6.cloned.1.call-done = bf16[512,256,32]{0,2,1:T(8,128)(2,1)} async-done(((bf16[512,2,32]{0,2,1:T(8,128)(2,1)}), bf16[512,256,32]{0,2,1:T(8,128)(2,1)}) %all-gather.6.cloned.1.call-update) | async-done | bytes 8388624 | tf_op jit(solution)/shard_map/all_gather | solution.py:116
  341.4 9.4 %fusion.26 = bf16[2,256,32,32]{2,3,0,1:T(8,128)(2,1)} fusion(bf16[512,256,32]{0,2,1:T(8,128)(2,1)} %all-gather.6.cloned.1.call-done, bf16[512,2,64]{0,2,1:T(8,128)(2,1)S(1)} %convolution_convert_fusion), kind=kOutput, calls=%fused_computation.30 | convolution fusion | flops 537919488 | bytes 9502720 | tf_op jit(solution)/shard_map/sic,sjd->ijcd/dot_general | solution.py:117
  350.8 6.2 %copy.71 = bf16[2,256,32,32]{1,3,2,0:T(8,128)(2,1)S(1)} copy(bf16[2,256,32,32]{2,3,0,1:T(8,128)(2,1)} %fusion.26) | data formatting | bytes 2097152 | tf_op jit(solution)/shard_map/convert_element_type | solution.py:118
  (141 shorter events, 88.3 us)
Async XLA Ops:
  7.2 58.2 %copy-start = (bf16[256,1024]{1,0:T(8,128)(2,1)S(1)}, bf16[256,1024]{1,0:T(8,128)(2,1)}, u32[]{:S(2)}) copy-start(bf16[256,1024]{1,0:T(8,128)(2,1)} %param.18) | copy-start | bytes 1572868
  7.2 91.6 %all-gather.4.cloned.1.call-start = ((), (), s32[]{:S(2)}) async-start(), calls=%async_computation.1 | async-start | bytes 1572864 | tf_op jit(solution)/shard_map/all_gather | solution.py:23
  67.4 3.0 copy-start.2
  67.4 1.1 copy-start.6
  100.9 37.8 %copy-start.3 = (bf16[4,256,256]{2,1,0:T(8,128)(2,1)S(1)}, bf16[4,256,256]{2,1,0:T(8,128)(2,1)}, u32[]{:S(2)}) copy-start(bf16[4,256,256]{2,1,0:T(8,128)(2,1)} %param.14) | copy-start | bytes 1572868
  101.0 37.8 %copy-start.9 = (bf16[256,256]{1,0:T(8,128)(2,1)S(1)}, bf16[256,256]{1,0:T(8,128)(2,1)}, u32[]{:S(2)}) copy-start(bf16[256,256]{1,0:T(8,128)(2,1)} %param.19) | copy-start | bytes 393220
  141.3 38.1 %copy-start.5 = (bf16[256,1024]{1,0:T(8,128)(2,1)S(1)}, bf16[256,1024]{1,0:T(8,128)(2,1)}, u32[]{:S(2)}) copy-start(bf16[256,1024]{1,0:T(8,128)(2,1)} %param.20) | copy-start | bytes 1572868
  141.3 33.6 %all-to-all-start = ((bf16[4,256,256]{2,0,1:T(4,128)(2,1)}), bf16[4,256,256]{2,0,1:T(4,128)(2,1)S(1)}, u32[]{:S(2)}, u32[]{:S(2)}) async-start(bf16[4,256,256]{2,0,1:T(4,128)(2,1)} %copy.59), calls=%async_computation | async-start | bytes 1048576 | tf_op jit(solution)/shard_map/all_to_all | solution.py:97
  155.8 185.6 %all-gather.6.cloned.1.call-start = ((), (), s32[]{:S(2)}) async-start(), calls=%async_computation.2 | async-start | bytes 8454144 | tf_op jit(solution)/shard_map/all_gather | solution.py:116
  180.1 1.9 copy-start.1
  186.6 74.9 %copy-start.8 = (bf16[256,256]{1,0:T(8,128)(2,1)S(1)}, bf16[256,256]{1,0:T(8,128)(2,1)}, u32[]{:S(2)}) copy-start(bf16[256,256]{1,0:T(8,128)(2,1)} %param.21) | copy-start | bytes 393220
  259.7 2.4 copy-start.10
  350.8 6.2 %copy-start.4 = (bf16[2,256,128]{2,1,0:T(8,128)(2,1)S(1)}, bf16[2,256,128]{2,1,0:T(8,128)(2,1)}, u32[]{:S(2)}) copy-start(bf16[2,256,128]{2,1,0:T(8,128)(2,1)} %param.15) | copy-start | bytes 393220
  350.8 6.2 %copy-start.7 = (bf16[1024,128]{1,0:T(8,128)(2,1)S(1)}, bf16[1024,128]{1,0:T(8,128)(2,1)}, u32[]{:S(2)}) copy-start(bf16[1024,128]{1,0:T(8,128)(2,1)} %param.23) | copy-start | bytes 786436
Sparse Core Ops, SparseCore 0:
  62.7 36.0 all-gather.3
  263.1 78.1 all-gather.5
where the time goes:
time: 368 us; the launch traced here: 365 us
  waiting for transfers between devices  124 us (34%)
  local copies, waits for them, and re-layouts  60.6 us (16%)
  matrix products  52.1 us (14%)
  blocking collectives  51.8 us (14%)
  Pallas kernels  30.7 us (8%)
  other arithmetic  16.8 us (5%)
  starting transfers between devices  14.8 us (4%)
  between operations  14.4 us (4%)
    all_gather x1, waiting for transfers between devices, shards(): piece = lax.all_gather(right, DAP, axis=1, tiled=True)  77.3 us
    all_gather x2, blocking collectives, stacked_from(): tiles = lax.all_gather(tiles, axes[k], axis=0, tiled=True)  51.8 us
    dot_general x8, Pallas kernels, one_head(): jnp.einsum('bij,bjd->bid', weights, vh, preferred_element_type=jnp.float32)  30.7 us
    all_gather x1, waiting for transfers between devices, stacked_from(): tiles = lax.all_gather(tiles, axes[k], axis=0, tiled=True)  27.3 us
    dynamic_slice x40, local copies, waits for them, and re-layouts, attend(): lax.map(one_head, (jnp.moveaxis(query, 2, 0), jnp.moveaxis(keys, 2, 0), j...  27.3 us
    all_to_all x1, waiting for transfers between devices, shards(): lax.all_to_all(homolog_later, DAP, split_axis=1, concat_axis=0, tiled=True)  18.9 us
    dynamic_update_slice x16, local copies, waits for them, and re-layouts, attend(): lax.map(one_head, (jnp.moveaxis(query, 2, 0), jnp.moveaxis(keys, 2, 0), j...  15 us
    dot_general x8, matrix products, one_head(): jnp.einsum('bij,bjd->bid', weights, vh, preferred_element_type=jnp.float32)  14.8 us
  transfers between devices with their start and end apart: 3, of which 3 were waited for; matrix products, arithmetic and copies ran while one was open for 2% of the time, Pallas kernels for 0%

commit v1 on v0

--- a/solution.py
+++ b/solution.py
@@ -11,6 +11,13 @@
 GROUPS_DAP = ("groups", "dap_0", "dap_1", "dap_2")
 
 
+def gather_over(array, name, dim):
+    size = lax.axis_size(name)
+    blocks = jnp.stack([array for _ in range(size)])
+    blocks = lax.all_to_all(blocks, name, split_axis=0, concat_axis=0)
+    return jnp.concatenate(blocks, axis=dim)
+
+
 def joined_along(tiles, dim):
     tiles = jnp.moveaxis(tiles, 0, dim)
     dims = tiles.shape
@@ -20,7 +27,7 @@
 def stacked_from(shard, axes, order):
     tiles = shard[None]
     for k in order:
-        tiles = lax.all_gather(tiles, axes[k], axis=0, tiled=True)
+        tiles = gather_over(tiles, axes[k], 0)
     carried = [lax.axis_size(axes[k]) for k in reversed(order)]
     tiles = tiles.reshape(*carried, *shard.shape)
     turned = sorted(range(len(order)), key=lambda place: order[len(order) - 1 - place])

time: 368 us -> 334 us (0.908)
  blocking collectives: 51.8 us -> 12.1 us
  starting transfers between devices: 14.8 us -> 29.9 us
  waiting for transfers between devices: 124 us -> 110 us
    all_gather x2 -> x0, blocking collectives: 51.8 us -> none  [stacked_from(): tiles = lax.all_gather(tiles, axes[k], axis=0, tiled=True)]
    all_gather x1 -> x0, waiting for transfers between devices: 27.3 us -> none  [stacked_from(): tiles = lax.all_gather(tiles, axes[k], axis=0, tiled=True)]
    all_to_all x0 -> x2, starting transfers between devices: none -> 20.8 us  [gather_over(): blocks = lax.all_to_all(blocks, name, split_axis=0, concat_axis=0)]
    all_to_all x0 -> x1, blocking collectives: none -> 12.1 us  [gather_over(): blocks = lax.all_to_all(blocks, name, split_axis=0, concat_axis=0)]
    all_gather x1, waiting for transfers between devices: 77.3 us -> 84.4 us  [shards(): piece = lax.all_gather(right, DAP, axis=1, tiled=True)]
    all_to_all x0 -> x2, waiting for transfers between devices: none -> 6.24 us  [gather_over(): blocks = lax.all_to_all(blocks, name, split_axis=0, concat_axis=0)]
    all_to_all x1, starting transfers between devices: 14.5 us -> 8.88 us  [shards(): lax.all_to_all(homolog_later, DAP, split_axis=1, concat_axis=0, tiled=True)]
  transfers between devices with their start and end apart: 3 -> 4, of which waited for: 3 -> 4; matrix products, arithmetic and copies ran while one was open for 2% -> 4% of each run, Pallas kernels for 0% -> 0%
where the time goes in v1:
time: 334 us; the launch traced here: 331 us
  waiting for transfers between devices  110 us (33%)
  local copies, waits for them, and re-layouts  60.1 us (18%)
  matrix products  54.1 us (16%)
  Pallas kernels  30.7 us (9%)
  starting transfers between devices  29.9 us (9%)
  other arithmetic  20.2 us (6%)
  between operations  14.4 us (4%)
  blocking collectives  12.1 us (4%)
    all_gather x1, waiting for transfers between devices, shards(): piece = lax.all_gather(right, DAP, axis=1, tiled=True)  84.4 us
    dot_general x8, Pallas kernels, one_head(): jnp.einsum('bij,bjd->bid', weights, vh, preferred_element_type=jnp.float32)  30.7 us
    dynamic_slice x40, local copies, waits for them, and re-layouts, attend(): lax.map(one_head, (jnp.moveaxis(query, 2, 0), jnp.moveaxis(keys, 2, 0), j...  27.3 us
    all_to_all x2, starting transfers between devices, gather_over(): blocks = lax.all_to_all(blocks, name, split_axis=0, concat_axis=0)  20.8 us
    all_to_all x1, waiting for transfers between devices, shards(): lax.all_to_all(homolog_later, DAP, split_axis=1, concat_axis=0, tiled=True)  18.9 us
    dynamic_update_slice x16, local copies, waits for them, and re-layouts, attend(): lax.map(one_head, (jnp.moveaxis(query, 2, 0), jnp.moveaxis(keys, 2, 0), j...  15 us
    dot_general x8, matrix products, one_head(): jnp.einsum('bij,bjd->bid', weights, vh, preferred_element_type=jnp.float32)  14.8 us
    all_to_all x1, blocking collectives, gather_over(): blocks = lax.all_to_all(blocks, name, split_axis=0, concat_axis=0)  12.1 us
  transfers between devices with their start and end apart: 4, of which 4 were waited for; matrix products, arithmetic and copies ran while one was open for 4% of the time, Pallas kernels for 0%

profile of v1, /device:TPU:513, one launch (start us, length us, event | category | flops | bytes accessed | tf_op | source)
XLA Modules:
  0.0 331.2 jit_solution(6684515352287282470)
XLA Ops:
  11.3 7.9 %all-to-all-start = ((bf16[8,1,8,2,256]{4,2,3,1,0:T(8,128)(2,1)}), bf16[8,1,8,2,256]{4,2,3,1,0:T(8,128)(2,1)S(1)}, u32[]{:S(2)}, u32[]{:S(2)}) async-start(bf16[8,1,8,2,256]{4,2,3,1,0:T(8,128)(2,1)} %stack.9), calls=%async_computation | async-start | bytes 131072 | tf_op jit(solution)/shard_map/all_to_all | solution.py:17
  21.9 4.5 %all-to-all-done = bf16[8,1,8,2,256]{4,2,3,1,0:T(8,128)(2,1)S(1)} async-done(((bf16[8,1,8,2,256]{4,2,3,1,0:T(8,128)(2,1)}), bf16[8,1,8,2,256]{4,2,3,1,0:T(8,128)(2,1)S(1)}, u32[]{:S(2)}, u32[]{:S(2)}) %all-to-all-start) | async-done | bytes 65568 | tf_op jit(solution)/shard_map/all_to_all | solution.py:17
  27.2 13.0 %all-to-all-start.1 = ((bf16[8,8,8,2,256]{4,2,3,1,0:T(8,128)(2,1)}), bf16[8,8,8,2,256]{4,2,3,1,0:T(8,128)(2,1)S(1)}, u32[]{:S(2)}, u32[]{:S(2)}) async-start(bf16[8,8,8,2,256]{4,2,3,1,0:T(8,128)(2,1)} %stack.10), calls=%async_computation.1 | async-start | bytes 1048576 | tf_op jit(solution)/shard_map/all_to_all | solution.py:17
  40.2 3.9 %fusion.59 = f32[4,256,1024]{1,2,0:T(8,128)} fusion(bf16[4,256,256]{2,1,0:T(8,128)(2,1)} %param.14, bf16[256,1024]{1,0:T(8,128)(2,1)S(1)} %copy-done, f32[4,256]{1,0:T(4,128)S(1)} %add_rsqrt_fusion.2, f32[4,256]{1,0:T(4,128)S(1)} %broadcast_multiply_fusion.2), kind=kOutput, calls=%fused_computation.77 | convolution fusion | flops 537919488 | bytes 5251072 | tf_op jit(solution)/shard_map/blc,cf->blf/dot_general | solution.py:50
  44.2 2.6 convert.20
  47.5 2.1 fusion.56
  52.6 12.1 %all_to_all.24 = bf16[2,64,8,2,256]{4,2,3,1,0:T(8,128)(2,1)S(1)} all-to-all(bf16[2,64,8,2,256]{4,2,3,1,0:T(8,128)(2,1)S(1)} %pad_maximum_fusion), channel_id=1, replica_groups=mesh['groups'=2,'dap_0'=8,'dap_1'=8,'dap_2'=2] {'dap_2'}, dimensions={0} | all-to-all | bytes 2097152 | tf_op jit(solution)/shard_map/all_to_all | solution.py:17
  65.6 36.0 %while.20 = (s32[]{:T(128)}, f32[8,4,256,32]{2,3,0,1:T(8,128)}, bf16[8,4,256,32]{2,3,0,1:T(8,128)(2,1)}, bf16[8,4,256,32]{2,3,0,1:T(8,128)(2,1)}, bf16[8,256,256...) while((s32[]{:T(128)}, f32[8,4,256,32]{2,3,0,1:T(8,128)}, ...), condition=%wide.region_7.8_spmd, body=%wide.region_4.7_spmd.sunk | while | flops 52233728 | bytes 4533337 | solution.py:66
  68.3 1.9 fusion.105
  72.8 1.9 fusion.105
  77.3 1.9 fusion.105
  81.8 1.8 fusion.105
  86.2 1.8 fusion.105
  90.7 1.8 fusion.105
  95.2 1.8 fusion.105
  99.7 1.9 fusion.105
  105.9 8.9 %all-to-all-start.3 = ((bf16[4,256,256]{2,0,1:T(4,128)(2,1)}), bf16[4,256,256]{2,0,1:T(4,128)(2,1)S(1)}, u32[]{:S(2)}, u32[]{:S(2)}) async-start(bf16[4,256,256]{2,0,1:T(4,128)(2,1)} %copy.81), calls=%async_computation.3 | async-start | bytes 1048576 | tf_op jit(solution)/shard_map/all_to_all | solution.py:104
  115.1 18.9 %all-to-all-done.3 = bf16[4,256,256]{2,0,1:T(4,128)(2,1)S(1)} async-done(((bf16[4,256,256]{2,0,1:T(4,128)(2,1)}), bf16[4,256,256]{2,0,1:T(4,128)(2,1)S(1)}, u32[]{:S(2)}, u32[]{:S(2)}) %all-to-all-start.3) | async-done | bytes 524320 | tf_op jit(solution)/shard_map/all_to_all | solution.py:104
  143.5 2.1 slice_bitcast_fusion
  145.6 73.0 %while.21 = (s32[]{:T(128)}, f32[8,2,512,32]{2,3,0,1:T(8,128)}, bf16[8,2,512,32]{2,3,0,1:T(8,128)(2,1)S(1)}, bf16[8,2,512,32]{2,3,0,1:T(8,128)(2,1)}, bf16[8,2,512,32]{2,3,0,1:T(8,128)(2,1)S(1)}, /*index=5*/s32[]{:T(128)}) while((s32[]{:T(128)}, f32[8,2,512,32]{2,3,0,1:T(8,128)}, bf16[8,2,512,32]{2,3,0,1:T(8,128)(2,1)S(1)}, ...), condition=%wide.region_13.14_spmd, body=%wide.region_10.13_spmd.sunk | while | flops 67108864 | bytes 1507417 | solution.py:66
  149.1 3.8 %dot_general.47 = f32[2,512,32]{2,1,0:T(8,128)} custom-call(bf16[2,512,32]{2,1,0:T(8,128)(2,1)} %bitcast.178, bf16[2,512,32]{2,1,0:T(8,128)(2,1)} %bitcast.177, bf16[2,512,32]{2,1,0:T(8,128)(2,1)} %bitcast.179), custom_call_target="tpu_custom_call" | custom-call | flops 67108864 | bytes 196608 | tf_op jit(solution)/shard_map/while/body/eval_jaxpr/bij,bjd->bid/dot_general | solution.py:64
  158.2 3.8 %dot_general.47 = f32[2,512,32]{2,1,0:T(8,128)} custom-call(bf16[2,512,32]{2,1,0:T(8,128)(2,1)} %bitcast.178, bf16[2,512,32]{2,1,0:T(8,128)(2,1)} %bitcast.177, bf16[2,512,32]{2,1,0:T(8,128)(2,1)} %bitcast.179), custom_call_target="tpu_custom_call" | custom-call | flops 67108864 | bytes 196608 | tf_op jit(solution)/shard_map/while/body/eval_jaxpr/bij,bjd->bid/dot_general | solution.py:64
  167.3 3.8 %dot_general.47 = f32[2,512,32]{2,1,0:T(8,128)} custom-call(bf16[2,512,32]{2,1,0:T(8,128)(2,1)} %bitcast.178, bf16[2,512,32]{2,1,0:T(8,128)(2,1)} %bitcast.177, bf16[2,512,32]{2,1,0:T(8,128)(2,1)} %bitcast.179), custom_call_target="tpu_custom_call" | custom-call | flops 67108864 | bytes 196608 | tf_op jit(solution)/shard_map/while/body/eval_jaxpr/bij,bjd->bid/dot_general | solution.py:64
  176.4 3.8 %dot_general.47 = f32[2,512,32]{2,1,0:T(8,128)} custom-call(bf16[2,512,32]{2,1,0:T(8,128)(2,1)} %bitcast.178, bf16[2,512,32]{2,1,0:T(8,128)(2,1)} %bitcast.177, bf16[2,512,32]{2,1,0:T(8,128)(2,1)} %bitcast.179), custom_call_target="tpu_custom_call" | custom-call | flops 67108864 | bytes 196608 | tf_op jit(solution)/shard_map/while/body/eval_jaxpr/bij,bjd->bid/dot_general | solution.py:64
  185.6 3.8 %dot_general.47 = f32[2,512,32]{2,1,0:T(8,128)} custom-call(bf16[2,512,32]{2,1,0:T(8,128)(2,1)} %bitcast.178, bf16[2,512,32]{2,1,0:T(8,128)(2,1)} %bitcast.177, bf16[2,512,32]{2,1,0:T(8,128)(2,1)} %bitcast.179), custom_call_target="tpu_custom_call" | custom-call | flops 67108864 | bytes 196608 | tf_op jit(solution)/shard_map/while/body/eval_jaxpr/bij,bjd->bid/dot_general | solution.py:64
  194.7 3.8 %dot_general.47 = f32[2,512,32]{2,1,0:T(8,128)} custom-call(bf16[2,512,32]{2,1,0:T(8,128)(2,1)} %bitcast.178, bf16[2,512,32]{2,1,0:T(8,128)(2,1)} %bitcast.177, bf16[2,512,32]{2,1,0:T(8,128)(2,1)} %bitcast.179), custom_call_target="tpu_custom_call" | custom-call | flops 67108864 | bytes 196608 | tf_op jit(solution)/shard_map/while/body/eval_jaxpr/bij,bjd->bid/dot_general | solution.py:64
  203.8 3.8 %dot_general.47 = f32[2,512,32]{2,1,0:T(8,128)} custom-call(bf16[2,512,32]{2,1,0:T(8,128)(2,1)} %bitcast.178, bf16[2,512,32]{2,1,0:T(8,128)(2,1)} %bitcast.177, bf16[2,512,32]{2,1,0:T(8,128)(2,1)} %bitcast.179), custom_call_target="tpu_custom_call" | custom-call | flops 67108864 | bytes 196608 | tf_op jit(solution)/shard_map/while/body/eval_jaxpr/bij,bjd->bid/dot_general | solution.py:64
  212.9 3.8 %dot_general.47 = f32[2,512,32]{2,1,0:T(8,128)} custom-call(bf16[2,512,32]{2,1,0:T(8,128)(2,1)} %bitcast.178, bf16[2,512,32]{2,1,0:T(8,128)(2,1)} %bitcast.177, bf16[2,512,32]{2,1,0:T(8,128)(2,1)} %bitcast.179), custom_call_target="tpu_custom_call" | custom-call | flops 67108864 | bytes 196608 | tf_op jit(solution)/shard_map/while/body/eval_jaxpr/bij,bjd->bid/dot_general | solution.py:64
  218.6 1.8 fusion.55
  223.1 84.4 %all-gather.2.cloned.1.call-done = bf16[512,256,32]{0,2,1:T(8,128)(2,1)} async-done(((bf16[512,2,32]{0,2,1:T(8,128)(2,1)}), bf16[512,256,32]{0,2,1:T(8,128)(2,1)}) %all-gather.2.cloned.1.call-update) | async-done | bytes 8388624 | tf_op jit(solution)/shard_map/all_gather | solution.py:123
  307.6 9.4 %fusion.26 = bf16[2,256,32,32]{2,3,0,1:T(8,128)(2,1)} fusion(bf16[512,256,32]{0,2,1:T(8,128)(2,1)} %all-gather.2.cloned.1.call-done, bf16[512,2,64]{0,2,1:T(8,128)(2,1)S(1)} %convolution_convert_fusion), kind=kOutput, calls=%fused_computation.30 | convolution fusion | flops 537919488 | bytes 9502720 | tf_op jit(solution)/shard_map/sic,sjd->ijcd/dot_general | solution.py:124
  317.0 6.2 %copy.93 = bf16[2,256,32,32]{1,3,2,0:T(8,128)(2,1)S(1)} copy(bf16[2,256,32,32]{2,3,0,1:T(8,128)(2,1)} %fusion.26) | data formatting | bytes 2097152 | tf_op jit(solution)/shard_map/convert_element_type | solution.py:125
  (142 shorter events, 93.4 us)
Async XLA Ops:
  7.2 33.0 %copy-start = (bf16[256,1024]{1,0:T(8,128)(2,1)S(1)}, bf16[256,1024]{1,0:T(8,128)(2,1)}, u32[]{:S(2)}) copy-start(bf16[256,1024]{1,0:T(8,128)(2,1)} %param.18) | copy-start | bytes 1572868
  11.3 15.1 %all-to-all-start = ((bf16[8,1,8,2,256]{4,2,3,1,0:T(8,128)(2,1)}), bf16[8,1,8,2,256]{4,2,3,1,0:T(8,128)(2,1)S(1)}, u32[]{:S(2)}, u32[]{:S(2)}) async-start(bf16[8,1,8,2,256]{4,2,3,1,0:T(8,128)(2,1)} %stack.9), calls=%async_computation | async-start | bytes 131072 | tf_op jit(solution)/shard_map/all_to_all | solution.py:17
  27.2 25.2 %all-to-all-start.1 = ((bf16[8,8,8,2,256]{4,2,3,1,0:T(8,128)(2,1)}), bf16[8,8,8,2,256]{4,2,3,1,0:T(8,128)(2,1)S(1)}, u32[]{:S(2)}, u32[]{:S(2)}) async-start(bf16[8,8,8,2,256]{4,2,3,1,0:T(8,128)(2,1)} %stack.10), calls=%async_computation.1 | async-start | bytes 1048576 | tf_op jit(solution)/shard_map/all_to_all | solution.py:17
  44.2 2.6 copy-start.5
  65.6 37.8 %copy-start.2 = (bf16[4,256,256]{2,1,0:T(8,128)(2,1)S(1)}, bf16[4,256,256]{2,1,0:T(8,128)(2,1)}, u32[]{:S(2)}) copy-start(bf16[4,256,256]{2,1,0:T(8,128)(2,1)} %param.14) | copy-start | bytes 1572868
  65.6 37.8 %copy-start.8 = (bf16[256,256]{1,0:T(8,128)(2,1)S(1)}, bf16[256,256]{1,0:T(8,128)(2,1)}, u32[]{:S(2)}) copy-start(bf16[256,256]{1,0:T(8,128)(2,1)} %param.19) | copy-start | bytes 393220
  105.9 32.4 %copy-start.4 = (bf16[256,1024]{1,0:T(8,128)(2,1)S(1)}, bf16[256,1024]{1,0:T(8,128)(2,1)}, u32[]{:S(2)}) copy-start(bf16[256,1024]{1,0:T(8,128)(2,1)} %param.20) | copy-start | bytes 1572868
  105.9 28.0 %all-to-all-start.3 = ((bf16[4,256,256]{2,0,1:T(4,128)(2,1)}), bf16[4,256,256]{2,0,1:T(4,128)(2,1)S(1)}, u32[]{:S(2)}, u32[]{:S(2)}) async-start(bf16[4,256,256]{2,0,1:T(4,128)(2,1)} %copy.81), calls=%async_computation.3 | async-start | bytes 1048576 | tf_op jit(solution)/shard_map/all_to_all | solution.py:104
  114.8 192.8 %all-gather.2.cloned.1.call-start = ((), (), s32[]{:S(2)}) async-start(), calls=%async_computation.4 | async-start | bytes 8454144 | tf_op jit(solution)/shard_map/all_gather | solution.py:123
  139.1 1.9 copy-start.1
  145.6 74.9 %copy-start.7 = (bf16[256,256]{1,0:T(8,128)(2,1)S(1)}, bf16[256,256]{1,0:T(8,128)(2,1)}, u32[]{:S(2)}) copy-start(bf16[256,256]{1,0:T(8,128)(2,1)} %param.21) | copy-start | bytes 393220
  218.6 2.4 copy-start.9
  317.0 6.2 %copy-start.3 = (bf16[2,256,128]{2,1,0:T(8,128)(2,1)S(1)}, bf16[2,256,128]{2,1,0:T(8,128)(2,1)}, u32[]{:S(2)}) copy-start(bf16[2,256,128]{2,1,0:T(8,128)(2,1)} %param.15) | copy-start | bytes 393220
  317.0 6.2 %copy-start.6 = (bf16[1024,128]{1,0:T(8,128)(2,1)S(1)}, bf16[1024,128]{1,0:T(8,128)(2,1)}, u32[]{:S(2)}) copy-start(bf16[1024,128]{1,0:T(8,128)(2,1)} %param.23) | copy-start | bytes 786436
Sparse Core Ops, SparseCore 0:
  222.1 85.3 all-gather.1
